TPU v7x, 32 devices: a whole 2x2x4 slice. The times are simulated.
32 devices in a mesh: sub: 8 (over z, y), dom: 4 (over x, core).
Axes of the slice: x: 2, y: 2, z: 4, core: 2. Of those that a mesh axis runs over, the one named last changes fastest.
Arguments:
- source_points: float32 [128, 3, 4096], P(('sub', 'dom')), may hold values from -4 to 4
- boundary: float32 [128, 8, 6, 128], P(('sub', 'dom')), may hold values from -4 to 4, as said below
- poses: float32 [12, 128], replicated, may hold values from -2 to 2, as said below
- anchor: float32 [128], P(('sub', 'dom')), may hold values from 0.3 to 3
- edge_target: int32 [128, 4], P(('sub', 'dom')), may hold values from 0 to 47, as said below
- corr_tile: int32 [128, 4, 4], P(('sub', 'dom')), may hold values from 0 to 7
- corr_source: int32 [128, 4, 4, 128], P(('sub', 'dom')), may hold values from 0 to 4095
- corr_lane: int32 [128, 4, 4, 128], P(('sub', 'dom')), may hold values from 0 to 127
Outputs:
- refined_pose: float32 [12, 128], P(None, ('sub', 'dom'))
Inputs may be any that keep to these rules, and one draw needn't show every extreme that they name: `poses`: each column holds a rotation matrix, row-major, followed by a translation. `boundary`: in every column of 6 entries the last 3 form a unit vector. `edge_target`: entry v of scan s names scan v % 16 of the previous (v // 16 = 0), the same (1) or the next (2) submap along the closed chain of submaps; it never names s itself; one scan may be named by several edges of s.
All inputs are finite; a program needn't handle non-finite values.
Results may differ from a plain program's by a relative error of at most 0.0001.
Values sent between devices are 32-bit elements; how exact they have to be, the bound alone decides.
No kernel may reach another device: no remote copies, remote signals or barrier semaphores. Data moves between devices by JAX's collectives and lax.ppermute only.
A program may use at most 64 MiB of HBM per device.

v0:
```python
import jax
import jax.numpy as jnp
from jax import lax
from jax.sharding import PartitionSpec as P

CG_ITERS = 2
GN_ITERS = 2
FINEST = lax.Precision.HIGHEST


def from_behind(block, axis, distance):
    devices = range(lax.axis_size(axis))
    route = [((i - distance) % len(devices), i) for i in devices]
    return lax.ppermute(block, axis, route)


def cayley(vector):
    first, second, third = (vector[0], vector[1], vector[2])
    length_sq = first * first + second * second + third * third
    inverse = 1.0 / (1.0 + length_sq)
    trace_part = 1.0 - length_sq
    entries = [
        [
            trace_part + 2.0 * first * first,
            2.0 * first * second - 2.0 * third,
            2.0 * first * third + 2.0 * second,
        ],
        [
            2.0 * first * second + 2.0 * third,
            trace_part + 2.0 * second * second,
            2.0 * second * third - 2.0 * first,
        ],
        [
            2.0 * first * third - 2.0 * second,
            2.0 * second * third + 2.0 * first,
            trace_part + 2.0 * third * third,
        ],
    ]
    return jnp.stack([jnp.stack(line) for line in entries]) * inverse


def rotate(matrix, vector):
    return jnp.stack(
        [
            matrix[row_id, 0] * vector[0]
            + matrix[row_id, 1] * vector[1]
            + matrix[row_id, 2] * vector[2]
            for row_id in range(3)
        ]
    )


def update(pose, increment):
    rotation = pose[:9].reshape(3, 3, -1)
    turn_mat = cayley(0.5 * increment[:3])
    rotated = jnp.stack(
        [
            jnp.stack(
                [
                    turn_mat[row_id, 0] * rotation[0, col_id]
                    + turn_mat[row_id, 1] * rotation[1, col_id]
                    + turn_mat[row_id, 2] * rotation[2, col_id]
                    for col_id in range(3)
                ]
            )
            for row_id in range(3)
        ]
    )
    moved_to = rotate(turn_mat, pose[9:]) + increment[3:]
    return jnp.concatenate([rotated.reshape(9, -1), moved_to], axis=0)


def scan_terms(points, pose_here, target_tiles, target_pose, sources, lane_ids):
    edge_count = sources.shape[0]
    picked = jnp.take(points, sources, axis=1)
    placed = rotate(pose_here[:9].reshape(3, 3), picked) + pose_here[9:, None, None, None]
    spread_lanes = jnp.broadcast_to(lane_ids[:, :, None, :], target_tiles.shape)
    chosen = jnp.take_along_axis(target_tiles, spread_lanes, axis=3)
    rotation = target_pose[:9].reshape(3, 3, edge_count)[:, :, :, None, None]
    shifted = target_pose[9:, :, None, None]
    target = (
        rotate(rotation, jnp.stack([chosen[:, :, 0], chosen[:, :, 1], chosen[:, :, 2]])) + shifted
    )
    normal = rotate(rotation, jnp.stack([chosen[:, :, 3], chosen[:, :, 4], chosen[:, :, 5]]))
    offset = target - placed
    misfit = normal[0] * offset[0] + normal[1] * offset[1] + normal[2] * offset[2]
    turned = jnp.stack(
        [
            placed[1] * normal[2] - placed[2] * normal[1],
            placed[2] * normal[0] - placed[0] * normal[2],
            placed[0] * normal[1] - placed[1] * normal[0],
        ]
    )
    jacobian = jnp.concatenate([turned, normal], axis=0).reshape(6, edge_count, -1)
    samples = jacobian.shape[2]
    blocks = jnp.einsum("aem,bem->eab", jacobian, jacobian, precision=FINEST) / samples
    slopes = (
        jnp.einsum("aem,em->ea", jacobian, misfit.reshape(edge_count, -1), precision=FINEST)
        / samples
    )
    return (blocks, slopes)


def window_order(sub_index, groups, scan_sub):
    slot_ids = (sub_index + jnp.arange(3, dtype=jnp.int32) - 1) % groups
    return (slot_ids[:, None] * scan_sub + jnp.arange(scan_sub, dtype=jnp.int32)[None, :]).reshape(
        -1
    )


def global_sum(value):
    return lax.psum(value, ("sub", "dom"))


def spread_out(own_part):
    pieces = [from_behind(own_part, "sub", offset_by) for offset_by in (1, -1)]
    before, middle, beyond = (
        lax.all_gather(pieces[0], "dom", axis=1, tiled=True),
        lax.all_gather(own_part, "dom", axis=1, tiled=True),
        lax.all_gather(pieces[1], "dom", axis=1, tiled=True),
    )
    nearby = jnp.concatenate([before, middle, beyond], axis=1)
    return nearby


def collect(partial_value):
    layers = partial_value.shape[0]
    scan_sub = partial_value.shape[2] // 3
    shared = lax.psum_scatter(
        partial_value.reshape(layers, 6, 3, scan_sub), "dom", scatter_dimension=3, tiled=True
    )
    summed = shared[:, :, 1]
    for slot_id, offset_by in ((0, -1), (2, 1)):
        summed = summed + from_behind(shared[:, :, slot_id], "sub", offset_by)
    return summed


def local(source_points, boundary, poses, anchor, edge_target, corr_tile, corr_source, corr_lane):
    scan_dev = source_points.shape[0]
    edge_count = edge_target.shape[1]
    groups = lax.axis_size("sub")
    scan_sub = scan_dev * lax.axis_size("dom")
    sub_index = lax.axis_index("sub")
    dom_index = lax.axis_index("dom")
    window_index = window_order(sub_index, groups, scan_sub)
    middle = lax.all_gather(boundary, "dom", axis=0, tiled=True)
    pieces = [from_behind(middle, "sub", offset_by) for offset_by in (1, -1)]
    window_tiles = jnp.concatenate([pieces[0], middle, pieces[1]], axis=0)
    window_pose = jnp.take(poses, window_index, axis=1)
    own_start = scan_sub + dom_index * scan_dev
    source_at = (own_start + jnp.arange(scan_dev, dtype=jnp.int32))[:, None] + jnp.zeros(
        (1, edge_count), jnp.int32
    )
    from_end = source_at.reshape(-1)
    to_end = edge_target.reshape(-1)
    win_width = 3 * scan_sub
    for turn_id in range(GN_ITERS):
        own_pose = lax.dynamic_slice_in_dim(window_pose, own_start, scan_dev, 1)

        def per_scan(per_item, window_pose=window_pose):
            points, pose_here, targets, tile_ids, sources, lane_ids = per_item
            return scan_terms(
                points,
                pose_here,
                window_tiles[targets[:, None], tile_ids],
                jnp.take(window_pose, targets, axis=1),
                sources,
                lane_ids,
            )

        blocks, slopes = lax.map(
            per_scan, (source_points, own_pose.T, edge_target, corr_tile, corr_source, corr_lane)
        )
        blocks = blocks.reshape(-1, 6, 6)
        slopes = slopes.reshape(-1, 6)
        diag_terms = jnp.diagonal(blocks, axis1=1, axis2=2)
        empty = jnp.zeros((6, win_width), jnp.float32)
        right_part = empty.at[:, from_end].add(slopes.T).at[:, to_end].add(-slopes.T)
        diag_part = empty.at[:, from_end].add(diag_terms.T).at[:, to_end].add(diag_terms.T)
        totals = collect(jnp.stack([right_part, diag_part]))
        right_side = totals[0]
        diagonal_sum = totals[1] + anchor[None, :]

        def apply_system(vector, blocks=blocks):
            nearby = spread_out(vector)
            spread = nearby[:, from_end] - nearby[:, to_end]
            pushed = jnp.einsum("kab,bk->ak", blocks, spread, precision=FINEST)
            partial_value = (
                jnp.zeros((6, win_width), jnp.float32)
                .at[:, from_end]
                .add(pushed)
                .at[:, to_end]
                .add(-pushed)
            )
            return collect(partial_value[None])[0] + anchor[None, :] * vector

        residual = right_side
        scaled = residual / diagonal_sum
        direction = scaled
        energy = global_sum(jnp.sum(residual * scaled))
        increment = jnp.zeros((6, scan_dev), jnp.float32)
        for sweep in range(CG_ITERS):
            image = apply_system(direction)
            step_len = energy / global_sum(jnp.sum(direction * image))
            increment = increment + step_len * direction
            residual = residual - step_len * image
            if sweep + 1 < CG_ITERS:
                scaled = residual / diagonal_sum
                renewed = global_sum(jnp.sum(residual * scaled))
                direction = scaled + renewed / energy * direction
                energy = renewed
        window_pose = update(window_pose, spread_out(increment))
    return lax.dynamic_slice_in_dim(window_pose, own_start, scan_dev, 1)


def solution(mesh):
    in_specs = (
        P(("sub", "dom"), None, None),
        P(("sub", "dom"), None, None, None),
        P(),
        P(("sub", "dom")),
        P(("sub", "dom"), None),
        P(("sub", "dom"), None, None),
        P(("sub", "dom"), None, None, None),
        P(("sub", "dom"), None, None, None),
    )
    out_specs = P(None, ("sub", "dom"))
    return jax.shard_map(local, mesh=mesh, in_specs=in_specs, out_specs=out_specs, check_vma=False)
```

profile of v0, /device:TPU:0, one launch (start us, length us, event | category | flops | bytes accessed | tf_op | source)
XLA Modules:
  0.0 1411.9 jit_solution(11835580075408723627)
XLA Ops:
  0.0 8.3 all_gather.57
  9.8 3.2 collective-permute-start.1
  15.1 5.6 copy.252
  22.1 5.0 collective-permute-done
  31.0 440.6 %while.24 = (s32[]{:T(128)}, f32[4,4,6,6]{3,1,0,2:T(4,128)S(1)}, f32[4,4,6]{2,1,0:T(4,128)S(1)}, f32[4,12]{1,0:T(4,128)S(1)}, f32[4,3,4096]{1,2,0:T(8,128)}, /*i...) while((s32[]{:T(128)}, f32[4,4,6,6]{3,1,0,2:T(4,128)S(1)}, ...), condition=%wide.region_1.5_spmd, body=%wide.region_0.0_spmd.sunk | while | flops 1492314 | bytes 1967897 | solution.py:171
  32.8 5.5 gather_fusion.3
  39.4 5.4 multiply_add_fusion.60
  47.1 91.5 %gather_fusion.1 = f32[12288]{0:T(1024)S(1)} fusion(f32[4,4,6,128]{3,2,1,0:T(8,128)S(1)} %bitcast.1328, s32[12288]{0:T(1024)S(1)} %reshape.2974), kind=kCustom, calls=%fused_computation.2.clone.clone.1 | custom fusion | bytes 294912 | tf_op jit(solution)/shard_map/while/body/eval_jaxpr/jit(take_along_axis)/gather | solution.py:78
  142.9 5.5 gather_fusion.3
  149.6 5.4 multiply_add_fusion.60
  157.2 91.5 %gather_fusion.1 = f32[12288]{0:T(1024)S(1)} fusion(f32[4,4,6,128]{3,2,1,0:T(8,128)S(1)} %bitcast.1328, s32[12288]{0:T(1024)S(1)} %reshape.2974), kind=kCustom, calls=%fused_computation.2.clone.clone.1 | custom fusion | bytes 294912 | tf_op jit(solution)/shard_map/while/body/eval_jaxpr/jit(take_along_axis)/gather | solution.py:78
  253.1 5.5 gather_fusion.3
  259.7 5.4 multiply_add_fusion.60
  267.4 91.5 %gather_fusion.1 = f32[12288]{0:T(1024)S(1)} fusion(f32[4,4,6,128]{3,2,1,0:T(8,128)S(1)} %bitcast.1328, s32[12288]{0:T(1024)S(1)} %reshape.2974), kind=kCustom, calls=%fused_computation.2.clone.clone.1 | custom fusion | bytes 294912 | tf_op jit(solution)/shard_map/while/body/eval_jaxpr/jit(take_along_axis)/gather | solution.py:78
  363.2 5.5 gather_fusion.3
  369.8 5.4 multiply_add_fusion.60
  377.5 91.5 %gather_fusion.1 = f32[12288]{0:T(1024)S(1)} fusion(f32[4,4,6,128]{3,2,1,0:T(8,128)S(1)} %bitcast.1328, s32[12288]{0:T(1024)S(1)} %reshape.2974), kind=kCustom, calls=%fused_computation.2.clone.clone.1 | custom fusion | bytes 294912 | tf_op jit(solution)/shard_map/while/body/eval_jaxpr/jit(take_along_axis)/gather | solution.py:78
  475.1 10.5 all-reduce
  485.7 3.6 collective-permute-start.2
  490.6 5.0 collective-permute-done.3
  497.7 5.2 all-gather.1
  502.9 5.2 all-gather.2
  508.1 5.2 all-gather
  516.1 11.0 all-reduce.1
  531.2 5.0 collective-permute-done.7
  537.0 37.1 %all-reduce.7 = (f32[]{:T(128)}, f32[]{:T(128)}) all-reduce(f32[]{:T(128)} %get-tuple-element.259, f32[]{:T(128)} %get-tuple-element.258), channel_id=1, replica_groups=mesh['sub'=8,'dom'=4] {'sub','dom'}, use_global_device_ids=true, to_apply=%region_8.12 | all-reduce | flops 2 | bytes 16 | tf_op jit(solution)/shard_map/psum | solution.py:112
  576.0 42.3 %psum.58 = f32[]{:T(128)} all-reduce(f32[]{:T(128)} %get-tuple-element.341), channel_id=1, replica_groups=mesh['sub'=8,'dom'=4] {'sub','dom'}, use_global_device_ids=true, to_apply=%region_15.19 | all-reduce | flops 1 | bytes 8 | tf_op jit(solution)/shard_map/psum | solution.py:112
  624.2 5.5 all-gather.4
  629.7 5.5 all-gather.3
  635.2 5.2 all-gather.5
  643.1 11.8 all-reduce.2
  662.0 36.9 %psum.59 = f32[]{:T(128)} all-reduce(f32[]{:T(128)} %fusion.120), channel_id=1, replica_groups=mesh['sub'=8,'dom'=4] {'sub','dom'}, use_global_device_ids=true, to_apply=%region_20.24 | all-reduce | flops 1 | bytes 8 | tf_op jit(solution)/shard_map/psum | solution.py:112
  704.9 5.5 all-gather.7
  710.4 5.5 all-gather.6
  716.0 5.4 all-gather.8
  722.0 440.6 %while.25 = (s32[]{:T(128)}, f32[4,4,6,6]{3,1,0,2:T(4,128)S(1)}, f32[4,4,6]{2,1,0:T(4,128)S(1)}, f32[4,12]{1,0:T(4,128)S(1)}, f32[4,3,4096]{1,2,0:T(8,128)}, /*i...) while((s32[]{:T(128)}, f32[4,4,6,6]{3,1,0,2:T(4,128)S(1)}, ...), condition=%wide.region_22.26_spmd, body=%wide.region_21.25_spmd.sunk | while | flops 1492314 | bytes 1967897 | solution.py:171
  723.8 5.5 gather_fusion.7
  730.5 5.4 multiply_add_fusion.62
  738.1 91.5 %gather_fusion.5 = f32[12288]{0:T(1024)S(1)} fusion(f32[4,4,6,128]{3,2,1,0:T(8,128)S(1)} %bitcast.1329, s32[12288]{0:T(1024)S(1)} %reshape.2987), kind=kCustom, calls=%fused_computation.6.clone.clone.1 | custom fusion | bytes 294912 | tf_op jit(solution)/shard_map/while/body/eval_jaxpr/jit(take_along_axis)/gather | solution.py:78
  834.0 5.5 gather_fusion.7
  840.6 5.4 multiply_add_fusion.62
  848.3 91.5 %gather_fusion.5 = f32[12288]{0:T(1024)S(1)} fusion(f32[4,4,6,128]{3,2,1,0:T(8,128)S(1)} %bitcast.1329, s32[12288]{0:T(1024)S(1)} %reshape.2987), kind=kCustom, calls=%fused_computation.6.clone.clone.1 | custom fusion | bytes 294912 | tf_op jit(solution)/shard_map/while/body/eval_jaxpr/jit(take_along_axis)/gather | solution.py:78
  944.1 5.5 gather_fusion.7
  950.7 5.4 multiply_add_fusion.62
  958.4 91.5 %gather_fusion.5 = f32[12288]{0:T(1024)S(1)} fusion(f32[4,4,6,128]{3,2,1,0:T(8,128)S(1)} %bitcast.1329, s32[12288]{0:T(1024)S(1)} %reshape.2987), kind=kCustom, calls=%fused_computation.6.clone.clone.1 | custom fusion | bytes 294912 | tf_op jit(solution)/shard_map/while/body/eval_jaxpr/jit(take_along_axis)/gather | solution.py:78
  1054.3 5.5 gather_fusion.7
  1060.9 5.4 multiply_add_fusion.62
  1068.6 91.5 %gather_fusion.5 = f32[12288]{0:T(1024)S(1)} fusion(f32[4,4,6,128]{3,2,1,0:T(8,128)S(1)} %bitcast.1329, s32[12288]{0:T(1024)S(1)} %reshape.2987), kind=kCustom, calls=%fused_computation.6.clone.clone.1 | custom fusion | bytes 294912 | tf_op jit(solution)/shard_map/while/body/eval_jaxpr/jit(take_along_axis)/gather | solution.py:78
  1166.2 12.1 all-reduce.3
  1184.8 4.7 collective-permute-start.17
  1189.6 5.2 all-gather.10
  1194.8 5.2 all-gather.9
  1200.0 5.2 all-gather.11
  1207.9 11.2 all-reduce.4
  1226.3 37.1 %all-reduce.6 = (f32[]{:T(128)}, f32[]{:T(128)}) all-reduce(f32[]{:T(128)} %get-tuple-element.257, f32[]{:T(128)} %get-tuple-element.256), channel_id=1, replica_groups=mesh['sub'=8,'dom'=4] {'sub','dom'}, use_global_device_ids=true, to_apply=%region_29.33 | all-reduce | flops 2 | bytes 16 | tf_op jit(solution)/shard_map/psum | solution.py:112
  1265.4 42.0 %psum.62 = f32[]{:T(128)} all-reduce(f32[]{:T(128)} %get-tuple-element.336), channel_id=1, replica_groups=mesh['sub'=8,'dom'=4] {'sub','dom'}, use_global_device_ids=true, to_apply=%region_36.40 | all-reduce | flops 1 | bytes 8 | tf_op jit(solution)/shard_map/psum | solution.py:112
  1313.4 5.5 all-gather.13
  1318.9 5.5 all-gather.12
  1324.4 5.2 all-gather.14
  1332.3 11.8 all-reduce.5
  1351.3 37.0 %psum.63 = f32[]{:T(128)} all-reduce(f32[]{:T(128)} %fusion.113), channel_id=1, replica_groups=mesh['sub'=8,'dom'=4] {'sub','dom'}, use_global_device_ids=true, to_apply=%region_41.45 | all-reduce | flops 1 | bytes 8 | tf_op jit(solution)/shard_map/psum | solution.py:112
  1394.5 5.5 all-gather.16
  1400.0 5.5 all-gather.15
  1405.6 5.2 all-gather.17
  (533 shorter events, 145.3 us)
Async XLA Ops:
  0.0 20.9 %copy-start.5 = (u32[32]{0:T(128)S(1)}, u32[32]{0:T(128)}, u32[]{:S(2)}) copy-start(u32[32]{0:T(128)} %constant.294) | copy-start | bytes 388
  0.0 20.9 %copy-start.4 = (s32[4,4]{1,0:T(4,128)S(1)}, s32[4,4]{1,0:T(4,128)}, u32[]{:S(2)}) copy-start(s32[4,4]{1,0:T(4,128)} %param.22) | copy-start | bytes 196
  8.3 18.8 %collective-permute-start = (f32[16,8,6,128]{3,1,2,0:T(8,128)S(1)}, f32[16,8,6,128]{3,1,2,0:T(8,128)S(1)}, u32[]{:S(2)}, u32[]{:S(2)}) collective-permute-start(f32[16,8,6,128]{3,1,2,0:T(8,128)S(1)} %all_gather.57), channel_id=1, source_target_pairs={{28,0},{0,4},{4,8},{8,12},{12,16},{16,20},{20,24},{24,28},{29,1},{... | collective-permute-start | bytes 1179656 | tf_op jit(solution)/shard_map/ppermute | solution.py:14
  9.8 19.5 %collective-permute-start.1 = (f32[16,8,6,128]{3,1,2,0:T(8,128)S(1)}, f32[16,8,6,128]{3,1,2,0:T(8,128)S(1)}, u32[]{:S(2)}, u32[]{:S(2)}) collective-permute-start(f32[16,8,6,128]{3,1,2,0:T(8,128)S(1)} %all_gather.57), channel_id=1, source_target_pairs={{4,0},{8,4},{12,8},{16,12},{20,16},{24,20},{28,24},{0,28},{5,1},{9... | collective-permute-start | bytes 1179656 | tf_op jit(solution)/shard_map/ppermute | solution.py:14
  15.1 15.9 %copy-start = (s32[4,4,4,128]{3,2,1,0:T(4,128)S(1)}, s32[4,4,4,128]{3,2,1,0:T(4,128)}, u32[]{:S(2)}) copy-start(s32[4,4,4,128]{3,2,1,0:T(4,128)} %param.24) | copy-start | bytes 98308
  15.1 15.9 %copy-start.1 = (s32[4,4,4,128]{3,2,1,0:T(4,128)S(1)}, s32[4,4,4,128]{3,2,1,0:T(4,128)}, u32[]{:S(2)}) copy-start(s32[4,4,4,128]{3,2,1,0:T(4,128)} %param.25) | copy-start | bytes 98308
  15.1 15.9 %copy-start.3 = (s32[4,4,4]{2,1,0:T(4,128)S(1)}, s32[4,4,4]{2,1,0:T(4,128)}, u32[]{:S(2)}) copy-start(s32[4,4,4]{2,1,0:T(4,128)} %param.23) | copy-start | bytes 772
  31.0 464.6 %copy-start.2 = (f32[4]{0:T(128)S(1)}, f32[4]{0:T(128)}, u32[]{:S(2)}) copy-start(f32[4]{0:T(128)} %param.21) | copy-start | bytes 52
  485.7 4.9 collective-permute-start.2
  489.3 6.3 collective-permute-start.3
  495.6 7.3 collective-permute-start.5
  495.7 12.5 collective-permute-start.4
  527.1 4.1 collective-permute-start.6
  529.9 6.3 collective-permute-start.7
  619.5 10.2 collective-permute-start.8
  622.0 13.2 collective-permute-start.9
  654.9 3.6 collective-permute-start.10
  655.0 6.3 collective-permute-start.11
  700.1 10.3 collective-permute-start.12
  702.6 13.4 collective-permute-start.13
  1178.3 3.7 collective-permute-start.14
  1178.4 6.4 collective-permute-start.15
  1184.8 10.0 collective-permute-start.16
  1184.8 15.2 %collective-permute-start.17 = (f32[6,4]{0,1:T(4,128)S(1)}, f32[6,4]{0,1:T(4,128)S(1)}, u32[]{:S(2)}, u32[]{:S(2)}) collective-permute-start(f32[6,4]{0,1:T(4,128)S(1)} %fusion.132), channel_id=1, source_target_pairs={{4,0},{8,4},{12,8},{16,12},{20,16},{24,20},{28,24},{0,28},{5,1},{9... | collective-permute-start | bytes 296 | tf_op jit(solution)/shard_map/ppermute | solution.py:14
  1219.2 3.6 collective-permute-start.18
  1219.2 6.3 collective-permute-start.19
  1308.7 10.2 collective-permute-start.20
  1311.2 13.2 collective-permute-start.21
  1344.1 3.6 collective-permute-start.22
  1344.2 6.3 collective-permute-start.23
  1389.7 10.3 collective-permute-start.24
  1392.3 13.3 collective-permute-start.25
where the time goes:
time: 1410 us
  local copies, waits for them, and re-layouts  843 us (60%)
  blocking collectives  405 us (29%)
  other arithmetic  67 us (5%)
  starting transfers between devices  45.1 us (3%)
  waiting for transfers between devices  36.7 us (3%)
    gather x24, local copies, waits for them, and re-layouts, scan_terms(): chosen = jnp.take_along_axis(target_tiles, spread_lanes, axis=3)  732 us
    psum x6, blocking collectives, global_sum(): return lax.psum(value, ('sub', 'dom'))  232 us
    unnamed x6, blocking collectives  68.4 us
    gather x16, local copies, waits for them, and re-layouts, scan_terms(): picked = jnp.take(points, sources, axis=1)  46.4 us
    add x26, other arithmetic, rotate(): matrix[row_id, 0] * vector[0] + matrix[row_id, 1] * vector[1]  45.1 us
    ppermute x26, starting transfers between devices, from_behind(): return lax.ppermute(block, axis, route)  45.1 us
    ppermute x26, waiting for transfers between devices, from_behind(): return lax.ppermute(block, axis, route)  36.7 us
    all_gather x6, blocking collectives, spread_out(): lax.all_gather(pieces[0], 'dom', axis=1, tiled=True)  32.2 us
  transfers between devices with their start and end apart: 26, of which 14 were waited for; matrix products, arithmetic and copies ran while one was open for 1% of the time, Pallas kernels for 0%

commit v1 on v0

--- a/solution.py
+++ b/solution.py
@@ -2,6 +2,7 @@
 import jax.numpy as jnp
 from jax import lax
 from jax.sharding import PartitionSpec as P
+from jax.lax import psum
 
 CG_ITERS = 2
 GN_ITERS = 2
@@ -109,7 +110,13 @@
 
 
 def global_sum(value):
-    return lax.psum(value, ("sub", "dom"))
+
+    def build_the_ladders(array_here):
+        for c in ("dom", "sub"):
+            array_here = psum(array_here, axis_name=c)
+        return array_here
+
+    return build_the_ladders(value)
 
 
 def spread_out(own_part):

time: 1410 us -> 1330 us (0.943)
  blocking collectives: 405 us -> 316 us
    psum x6 -> x12, blocking collectives: 232 us -> 148 us  [build_the_ladders(): array_here = psum(array_here, axis_name=c)]
where the time goes in v1:
time: 1330 us; the launch traced here: 1320 us
  local copies, waits for them, and re-layouts  843 us (63%)
  blocking collectives  316 us (24%)
  other arithmetic  66.8 us (5%)
  starting transfers between devices  45.1 us (3%)
  waiting for transfers between devices  36.7 us (3%)
    gather x24, local copies, waits for them, and re-layouts, scan_terms(): chosen = jnp.take_along_axis(target_tiles, spread_lanes, axis=3)  732 us
    psum x12, blocking collectives, build_the_ladders(): array_here = psum(array_here, axis_name=c)  148 us
    unnamed x6, blocking collectives  66.2 us
    gather x16, local copies, waits for them, and re-layouts, scan_terms(): picked = jnp.take(points, sources, axis=1)  46.4 us
    add x26, other arithmetic, rotate(): matrix[row_id, 0] * vector[0] + matrix[row_id, 1] * vector[1]  45.1 us
    ppermute x26, starting transfers between devices, from_behind(): return lax.ppermute(block, axis, route)  45.1 us
    ppermute x26, waiting for transfers between devices, from_behind(): return lax.ppermute(block, axis, route)  36.7 us
    all_gather x6, blocking collectives, spread_out(): lax.all_gather(pieces[1], 'dom', axis=1, tiled=True)  31.3 us
  transfers between devices with their start and end apart: 26, of which 14 were waited for; matrix products, arithmetic and copies ran while one was open for 1% of the time, Pallas kernels for 0%

profile of v1, /device:TPU:0, one launch (start us, length us, event | category | flops | bytes accessed | tf_op | source)
XLA Modules:
  0.0 1323.5 jit_solution(17063593063039120895)
XLA Ops:
  0.0 8.3 all_gather.57
  15.1 5.6 copy.252
  31.0 440.6 %while.24 = (s32[]{:T(128)}, f32[4,4,6,6]{3,1,0,2:T(4,128)S(1)}, f32[4,4,6]{2,1,0:T(4,128)S(1)}, f32[4,12]{1,0:T(4,128)S(1)}, f32[4,3,4096]{1,2,0:T(8,128)}, /*i...) while((s32[]{:T(128)}, f32[4,4,6,6]{3,1,0,2:T(4,128)S(1)}, ...), condition=%wide.region_1.5_spmd, body=%wide.region_0.0_spmd.sunk | while | flops 1492314 | bytes 1967897 | solution.py:178
  32.8 5.5 gather_fusion.3
  39.4 5.4 multiply_add_fusion.60
  47.1 91.5 %gather_fusion.1 = f32[12288]{0:T(1024)S(1)} fusion(f32[4,4,6,128]{3,2,1,0:T(8,128)S(1)} %bitcast.1328, s32[12288]{0:T(1024)S(1)} %reshape.2974), kind=kCustom, calls=%fused_computation.2.clone.clone.1 | custom fusion | bytes 294912 | tf_op jit(solution)/shard_map/while/body/eval_jaxpr/jit(take_along_axis)/gather | solution.py:79
  142.9 5.5 gather_fusion.3
  149.6 5.4 multiply_add_fusion.60
  157.2 91.5 %gather_fusion.1 = f32[12288]{0:T(1024)S(1)} fusion(f32[4,4,6,128]{3,2,1,0:T(8,128)S(1)} %bitcast.1328, s32[12288]{0:T(1024)S(1)} %reshape.2974), kind=kCustom, calls=%fused_computation.2.clone.clone.1 | custom fusion | bytes 294912 | tf_op jit(solution)/shard_map/while/body/eval_jaxpr/jit(take_along_axis)/gather | solution.py:79
  253.1 5.5 gather_fusion.3
  259.7 5.4 multiply_add_fusion.60
  267.4 91.5 %gather_fusion.1 = f32[12288]{0:T(1024)S(1)} fusion(f32[4,4,6,128]{3,2,1,0:T(8,128)S(1)} %bitcast.1328, s32[12288]{0:T(1024)S(1)} %reshape.2974), kind=kCustom, calls=%fused_computation.2.clone.clone.1 | custom fusion | bytes 294912 | tf_op jit(solution)/shard_map/while/body/eval_jaxpr/jit(take_along_axis)/gather | solution.py:79
  363.2 5.5 gather_fusion.3
  369.8 5.4 multiply_add_fusion.60
  377.5 91.5 %gather_fusion.1 = f32[12288]{0:T(1024)S(1)} fusion(f32[4,4,6,128]{3,2,1,0:T(8,128)S(1)} %bitcast.1328, s32[12288]{0:T(1024)S(1)} %reshape.2974), kind=kCustom, calls=%fused_computation.2.clone.clone.1 | custom fusion | bytes 294912 | tf_op jit(solution)/shard_map/while/body/eval_jaxpr/jit(take_along_axis)/gather | solution.py:79
  475.1 10.5 all-reduce
  497.7 5.2 all-gather.1
  502.9 5.2 all-gather.2
  508.1 5.2 all-gather
  516.1 11.0 all-reduce.1
  536.9 6.3 all-reduce.9
  543.2 17.8 %all-reduce.7 = (f32[]{:T(128)}, f32[]{:T(128)}) all-reduce(f32[]{:T(128)} %get-tuple-element.310, f32[]{:T(128)} %get-tuple-element.311), channel_id=1, replica_groups=mesh['sub'=8,'dom'=4] {'sub'}, use_global_device_ids=true, to_apply=%region_9.13 | all-reduce | flops 2 | bytes 16 | tf_op jit(solution)/shard_map/psum | solution.py:116
  562.8 6.3 psum.116
  569.2 19.8 %psum.117 = f32[]{:T(128)} all-reduce(f32[]{:T(128)} %psum.116), channel_id=1, replica_groups=mesh['sub'=8,'dom'=4] {'sub'}, use_global_device_ids=true, to_apply=%region_18.22 | all-reduce | flops 1 | bytes 8 | tf_op jit(solution)/shard_map/psum | solution.py:116
  595.1 5.2 all-gather.4
  600.3 5.2 all-gather.3
  605.5 5.2 all-gather.5
  613.4 11.1 all-reduce.2
  631.6 6.2 psum.118
  637.8 17.7 %psum.119 = f32[]{:T(128)} all-reduce(f32[]{:T(128)} %psum.118), channel_id=1, replica_groups=mesh['sub'=8,'dom'=4] {'sub'}, use_global_device_ids=true, to_apply=%region_24.28 | all-reduce | flops 1 | bytes 8 | tf_op jit(solution)/shard_map/psum | solution.py:116
  661.6 5.2 all-gather.7
  666.9 5.2 all-gather.6
  672.2 5.4 all-gather.8
  678.3 440.6 %while.25 = (s32[]{:T(128)}, f32[4,4,6,6]{3,1,0,2:T(4,128)S(1)}, f32[4,4,6]{2,1,0:T(4,128)S(1)}, f32[4,12]{1,0:T(4,128)S(1)}, f32[4,3,4096]{1,2,0:T(8,128)}, /*i...) while((s32[]{:T(128)}, f32[4,4,6,6]{3,1,0,2:T(4,128)S(1)}, ...), condition=%wide.region_26.30_spmd, body=%wide.region_25.29_spmd.sunk | while | flops 1492314 | bytes 1967897 | solution.py:178
  680.0 5.5 gather_fusion.7
  686.7 5.4 multiply_add_fusion.62
  694.3 91.5 %gather_fusion.5 = f32[12288]{0:T(1024)S(1)} fusion(f32[4,4,6,128]{3,2,1,0:T(8,128)S(1)} %bitcast.1329, s32[12288]{0:T(1024)S(1)} %reshape.2987), kind=kCustom, calls=%fused_computation.6.clone.clone.1 | custom fusion | bytes 294912 | tf_op jit(solution)/shard_map/while/body/eval_jaxpr/jit(take_along_axis)/gather | solution.py:79
  790.2 5.5 gather_fusion.7
  796.8 5.4 multiply_add_fusion.62
  804.5 91.5 %gather_fusion.5 = f32[12288]{0:T(1024)S(1)} fusion(f32[4,4,6,128]{3,2,1,0:T(8,128)S(1)} %bitcast.1329, s32[12288]{0:T(1024)S(1)} %reshape.2987), kind=kCustom, calls=%fused_computation.6.clone.clone.1 | custom fusion | bytes 294912 | tf_op jit(solution)/shard_map/while/body/eval_jaxpr/jit(take_along_axis)/gather | solution.py:79
  900.3 5.5 gather_fusion.7
  907.0 5.4 multiply_add_fusion.62
  914.6 91.5 %gather_fusion.5 = f32[12288]{0:T(1024)S(1)} fusion(f32[4,4,6,128]{3,2,1,0:T(8,128)S(1)} %bitcast.1329, s32[12288]{0:T(1024)S(1)} %reshape.2987), kind=kCustom, calls=%fused_computation.6.clone.clone.1 | custom fusion | bytes 294912 | tf_op jit(solution)/shard_map/while/body/eval_jaxpr/jit(take_along_axis)/gather | solution.py:79
  1010.5 5.5 gather_fusion.7
  1017.1 5.4 multiply_add_fusion.62
  1024.8 91.5 %gather_fusion.5 = f32[12288]{0:T(1024)S(1)} fusion(f32[4,4,6,128]{3,2,1,0:T(8,128)S(1)} %bitcast.1329, s32[12288]{0:T(1024)S(1)} %reshape.2987), kind=kCustom, calls=%fused_computation.6.clone.clone.1 | custom fusion | bytes 294912 | tf_op jit(solution)/shard_map/while/body/eval_jaxpr/jit(take_along_axis)/gather | solution.py:79
  1122.4 11.4 all-reduce.3
  1145.1 5.2 all-gather.10
  1150.3 5.2 all-gather.9
  1155.5 5.2 all-gather.11
  1163.4 11.1 all-reduce.4
  1181.6 6.3 all-reduce.8
  1188.0 17.8 %all-reduce.6 = (f32[]{:T(128)}, f32[]{:T(128)}) all-reduce(f32[]{:T(128)} %get-tuple-element.308, f32[]{:T(128)} %get-tuple-element.309), channel_id=1, replica_groups=mesh['sub'=8,'dom'=4] {'sub'}, use_global_device_ids=true, to_apply=%region_34.38 | all-reduce | flops 2 | bytes 16 | tf_op jit(solution)/shard_map/psum | solution.py:116
  1207.7 6.3 psum.124
  1213.9 19.7 %psum.125 = f32[]{:T(128)} all-reduce(f32[]{:T(128)} %psum.124), channel_id=1, replica_groups=mesh['sub'=8,'dom'=4] {'sub'}, use_global_device_ids=true, to_apply=%region_43.47 | all-reduce | flops 1 | bytes 8 | tf_op jit(solution)/shard_map/psum | solution.py:116
  1239.7 5.2 all-gather.13
  1244.9 5.2 all-gather.12
  1250.1 5.2 all-gather.14
  1258.1 11.0 all-reduce.5
  1276.3 6.3 psum.126
  1282.6 17.8 %psum.127 = f32[]{:T(128)} all-reduce(f32[]{:T(128)} %psum.126), channel_id=1, replica_groups=mesh['sub'=8,'dom'=4] {'sub'}, use_global_device_ids=true, to_apply=%region_49.53 | all-reduce | flops 1 | bytes 8 | tf_op jit(solution)/shard_map/psum | solution.py:116
  1306.6 5.2 all-gather.16
  1311.9 5.2 all-gather.15
  1317.1 5.2 all-gather.17
  (539 shorter events, 171.5 us)
Async XLA Ops:
  0.0 20.9 %copy-start.5 = (u32[32]{0:T(128)S(1)}, u32[32]{0:T(128)}, u32[]{:S(2)}) copy-start(u32[32]{0:T(128)} %constant.294) | copy-start | bytes 388
  0.0 20.9 %copy-start.4 = (s32[4,4]{1,0:T(4,128)S(1)}, s32[4,4]{1,0:T(4,128)}, u32[]{:S(2)}) copy-start(s32[4,4]{1,0:T(4,128)} %param.22) | copy-start | bytes 196
  8.3 18.8 %collective-permute-start = (f32[16,8,6,128]{3,1,2,0:T(8,128)S(1)}, f32[16,8,6,128]{3,1,2,0:T(8,128)S(1)}, u32[]{:S(2)}, u32[]{:S(2)}) collective-permute-start(f32[16,8,6,128]{3,1,2,0:T(8,128)S(1)} %all_gather.57), channel_id=1, source_target_pairs={{28,0},{0,4},{4,8},{8,12},{12,16},{16,20},{20,24},{24,28},{29,1},{... | collective-permute-start | bytes 1179656 | tf_op jit(solution)/shard_map/ppermute | solution.py:15
  9.8 19.5 %collective-permute-start.1 = (f32[16,8,6,128]{3,1,2,0:T(8,128)S(1)}, f32[16,8,6,128]{3,1,2,0:T(8,128)S(1)}, u32[]{:S(2)}, u32[]{:S(2)}) collective-permute-start(f32[16,8,6,128]{3,1,2,0:T(8,128)S(1)} %all_gather.57), channel_id=1, source_target_pairs={{4,0},{8,4},{12,8},{16,12},{20,16},{24,20},{28,24},{0,28},{5,1},{9... | collective-permute-start | bytes 1179656 | tf_op jit(solution)/shard_map/ppermute | solution.py:15
  15.1 15.9 %copy-start = (s32[4,4,4,128]{3,2,1,0:T(4,128)S(1)}, s32[4,4,4,128]{3,2,1,0:T(4,128)}, u32[]{:S(2)}) copy-start(s32[4,4,4,128]{3,2,1,0:T(4,128)} %param.24) | copy-start | bytes 98308
  15.1 15.9 %copy-start.1 = (s32[4,4,4,128]{3,2,1,0:T(4,128)S(1)}, s32[4,4,4,128]{3,2,1,0:T(4,128)}, u32[]{:S(2)}) copy-start(s32[4,4,4,128]{3,2,1,0:T(4,128)} %param.25) | copy-start | bytes 98308
  15.1 15.9 %copy-start.3 = (s32[4,4,4]{2,1,0:T(4,128)S(1)}, s32[4,4,4]{2,1,0:T(4,128)}, u32[]{:S(2)}) copy-start(s32[4,4,4]{2,1,0:T(4,128)} %param.23) | copy-start | bytes 772
  31.0 464.6 %copy-start.2 = (f32[4]{0:T(128)S(1)}, f32[4]{0:T(128)}, u32[]{:S(2)}) copy-start(f32[4]{0:T(128)} %param.21) | copy-start | bytes 52
  485.7 4.9 collective-permute-start.2
  489.3 6.3 collective-permute-start.3
  495.6 7.3 collective-permute-start.5
  495.7 12.5 collective-permute-start.4
  527.1 4.1 collective-permute-start.6
  529.9 6.3 collective-permute-start.7
  590.4 9.9 collective-permute-start.8
  590.4 15.1 %collective-permute-start.9 = (f32[6,4]{0,1:T(4,128)S(1)}, f32[6,4]{0,1:T(4,128)S(1)}, u32[]{:S(2)}, u32[]{:S(2)}) collective-permute-start(f32[6,4]{0,1:T(4,128)S(1)} %multiply_add_fusion.21), channel_id=1, source_target_pairs={{4,0},{8,4},{12,8},{16,12},{20,16},{24,20},{28,24},{0,28},{5,1},{9... | collective-permute-start | bytes 296 | tf_op jit(solution)/shard_map/ppermute | solution.py:15
  624.6 3.6 collective-permute-start.10
  624.6 6.3 collective-permute-start.11
  656.9 10.0 collective-permute-start.12
  658.9 13.2 %collective-permute-start.13 = (f32[6,4]{0,1:T(4,128)S(1)}, f32[6,4]{0,1:T(4,128)S(1)}, u32[]{:S(2)}, u32[]{:S(2)}) collective-permute-start(f32[6,4]{0,1:T(4,128)S(1)} %multiply_add_fusion.20), channel_id=1, source_target_pairs={{4,0},{8,4},{12,8},{16,12},{20,16},{24,20},{28,24},{0,28},{5,1},{9... | collective-permute-start | bytes 296 | tf_op jit(solution)/shard_map/ppermute | solution.py:15
  1133.8 3.7 collective-permute-start.14
  1133.9 6.4 collective-permute-start.15
  1140.3 10.0 collective-permute-start.16
  1140.3 15.2 %collective-permute-start.17 = (f32[6,4]{0,1:T(4,128)S(1)}, f32[6,4]{0,1:T(4,128)S(1)}, u32[]{:S(2)}, u32[]{:S(2)}) collective-permute-start(f32[6,4]{0,1:T(4,128)S(1)} %fusion.132), channel_id=1, source_target_pairs={{4,0},{8,4},{12,8},{16,12},{20,16},{24,20},{28,24},{0,28},{5,1},{9... | collective-permute-start | bytes 296 | tf_op jit(solution)/shard_map/ppermute | solution.py:15
  1174.6 3.6 collective-permute-start.18
  1174.6 6.3 collective-permute-start.19
  1235.0 9.9 collective-permute-start.20
  1235.0 15.1 %collective-permute-start.21 = (f32[6,4]{0,1:T(4,128)S(1)}, f32[6,4]{0,1:T(4,128)S(1)}, u32[]{:S(2)}, u32[]{:S(2)}) collective-permute-start(f32[6,4]{0,1:T(4,128)S(1)} %multiply_add_fusion.19), channel_id=1, source_target_pairs={{4,0},{8,4},{12,8},{16,12},{20,16},{24,20},{28,24},{0,28},{5,1},{9... | collective-permute-start | bytes 296 | tf_op jit(solution)/shard_map/ppermute | solution.py:15
  1269.1 3.6 collective-permute-start.22
  1269.2 6.3 collective-permute-start.23
  1301.9 10.0 collective-permute-start.24
  1303.9 13.2 %collective-permute-start.25 = (f32[6,4]{0,1:T(4,128)S(1)}, f32[6,4]{0,1:T(4,128)S(1)}, u32[]{:S(2)}, u32[]{:S(2)}) collective-permute-start(f32[6,4]{0,1:T(4,128)S(1)} %multiply_add_fusion.18), channel_id=1, source_target_pairs={{4,0},{8,4},{12,8},{16,12},{20,16},{24,20},{28,24},{0,28},{5,1},{9... | collective-permute-start | bytes 296 | tf_op jit(solution)/shard_map/ppermute | solution.py:15
